TPU v7x, 512 devices: a 8x2x16 block of a 8x8x16 slice. The times are simulated.
512 devices in a mesh: groups: 2 (over y), mp: 16 (over z), dp: 8 (over x), guide: 2 (over core).
Axes of the slice: x: 8, y: 2, z: 16, core: 2. Of those that a mesh axis runs over, the one named last changes fastest.
The devices are a block of a 8x8x16 slice.
Arguments:
- tokens: bfloat16 [768, 8192], P(('groups', 'mp'), ('dp', 'guide')), parts along dimension 0, may hold values from -6 to 6
- w_gate: bfloat16 [8192, 14336], P(('dp', 'guide'), 'mp'), may hold values from -0.0625 to 0.0625
- w_up: bfloat16 [8192, 14336], P(('dp', 'guide'), 'mp'), may hold values from -0.0625 to 0.0625
- w_down: bfloat16 [14336, 8192], P('mp', ('dp', 'guide')), may hold values from -0.046875 to 0.046875
Outputs:
- layer_output: bfloat16 [768, 8192], P(('groups', 'mp'), ('dp', 'guide')), parts along dimension 0
There are 2 independent parts, one for each index of `groups`. A program takes and returns all parts, laid end to end along the dimension named above; an argument that names none is the same for every part. Nothing has to cross between parts.
All inputs are finite; a program needn't handle non-finite values.
Results may differ from a plain program's by a relative error of at most 0.0049.
Values may be sent and summed in bfloat16 or wider, within the bound.
No kernel may reach another device: no remote copies, remote signals or barrier semaphores. Data moves between devices by JAX's collectives and lax.ppermute only.
A program may use at most 64 MiB of HBM per device.

v0:
```python
import jax
import jax.numpy as jnp
from jax import lax
from jax.sharding import PartitionSpec as P


def summed_on_arrival(tiles, axis):
    arrived = lax.all_to_all(tiles, axis, split_axis=0, concat_axis=0, tiled=True)
    return arrived.astype(jnp.float32).sum(axis=0)


def cut(shard, count):
    return shard.reshape(count, shard.shape[0] // count, *shard.shape[1:])


def per_device(tokens, w_gate, w_up, w_down):
    columns = w_gate.shape[1]
    mp, dp, guide = (lax.axis_size(axis) for axis in ("mp", "dp", "guide"))
    paired_weights = jnp.concatenate([w_gate, w_up], axis=1)
    blocks = lax.all_gather(tokens, "mp", axis=0, tiled=False)
    blocks = blocks.reshape(dp, guide, -1, *tokens.shape)
    gathered = blocks.swapaxes(0, 1).reshape(-1, tokens.shape[1])
    partial_terms = jnp.dot(gathered, paired_weights, preferred_element_type=jnp.float32)
    chip_terms = summed_on_arrival(cut(partial_terms, guide), "guide").astype(jnp.bfloat16)
    summed = summed_on_arrival(cut(chip_terms, dp), "dp")
    hidden_share = (jax.nn.silu(summed[:, :columns]) * summed[:, columns:]).astype(jnp.bfloat16)
    hidden = lax.all_gather(hidden_share, ("dp", "guide"), axis=0, tiled=True)
    output_terms = jnp.dot(hidden, w_down, preferred_element_type=jnp.float32).astype(jnp.bfloat16)
    return summed_on_arrival(cut(output_terms, mp), "mp").astype(jnp.bfloat16)


def solution(mesh):
    placed = (
        P(("groups", "mp"), ("dp", "guide")),
        P(("dp", "guide"), "mp"),
        P(("dp", "guide"), "mp"),
        P("mp", ("dp", "guide")),
    )
    return jax.shard_map(
        per_device,
        mesh=mesh,
        in_specs=placed,
        out_specs=P(("groups", "mp"), ("dp", "guide")),
        check_vma=False,
    )
```

profile of v0, /device:TPU:80, one launch (start us, length us, event | category | flops | bytes accessed | tf_op | source)
XLA Modules:
  0.0 155.5 jit_solution(7631162222626804880)
XLA Ops:
  0.0 0.0 copy-start
  0.0 70.5 %all-gather = bf16[384,512]{1,0:T(8,128)(2,1)S(1)} all-gather(bf16[24,512]{1,0:T(8,128)(2,1)} %param.4), channel_id=2, replica_groups=mesh['groups'=2,'mp'=16,'dp'=8,'guide'=2] {'mp'}, dimensions={0}, use_global_device_ids=true | all-gather | bytes 417792 | tf_op jit(solution)/shard_map/all_gather | solution.py:20
  70.6 2.3 %fusion = f32[1792,384]{0,1:T(8,128)S(1)} fusion(bf16[384,512]{1,0:T(8,128)(2,1)S(1)} %bitcast.14, bf16[512,896]{1,0:T(8,128)(2,1)} %param.6, bf16[512,896]{1,0:T(8,128)(2,1)} %param.5), kind=kOutput, calls=%fused_computation | convolution fusion | flops 708313088 | bytes 4980736 | tf_op jit(solution)/shard_map/dot_general | solution.py:23
  72.9 6.9 %all_to_all.15 = f32[2,192,1792]{2,1,0:T(8,128)} all-to-all(f32[2,192,1792]{2,1,0:T(8,128)S(1)} %bitcast.12), channel_id=1, replica_groups=mesh['groups'=2,'mp'=16,'dp'=8,'guide'=2] {'guide'}, dimensions={0} | all-to-all | bytes 5505024 | tf_op jit(solution)/shard_map/all_to_all | solution.py:8
  79.8 2.0 %reduce_sum.30 = bf16[192,1792]{1,0:T(8,128)(2,1)S(1)} reduce(f32[2,192,1792]{2,1,0:T(8,128)} %all_to_all.15, f32[]{:T(128)} %constant.4.clone.1), dimensions={0}, to_apply=%region_0.0 | reduce | flops 344064 | bytes 3440644 | tf_op jit(solution)/shard_map/reduce_sum | solution.py:9
  81.8 28.4 %all_to_all.16 = bf16[8,24,1792]{2,1,0:T(8,128)(2,1)S(1)} all-to-all(bf16[8,24,1792]{2,1,0:T(8,128)(2,1)S(1)} %bitcast.13), channel_id=1, replica_groups=mesh['groups'=2,'mp'=16,'dp'=8,'guide'=2] {'dp'}, dimensions={0} | all-to-all | bytes 1376256 | tf_op jit(solution)/shard_map/all_to_all | solution.py:8
  110.2 0.1 convert_reduce_fusion
  110.4 16.6 %all_gather.11 = bf16[384,896]{1,0:T(8,128)(2,1)S(1)} all-gather(bf16[24,896]{1,0:T(8,128)(2,1)S(1)} %fusion.4), channel_id=1, replica_groups=mesh['groups'=2,'mp'=16,'dp'=8,'guide'=2] {'dp','guide'}, dimensions={0}, use_global_device_ids=true | all-gather | bytes 731136 | tf_op jit(solution)/shard_map/all_gather | solution.py:27
  127.0 0.0 copy-done
  127.0 0.6 convolution_convert_fusion
  127.6 27.3 %all_to_all.17 = bf16[16,24,512]{2,1,0:T(8,128)(2,1)S(1)} all-to-all(bf16[16,24,512]{2,1,0:T(8,128)(2,1)S(1)} %bitcast.16), channel_id=1, replica_groups=mesh['groups'=2,'mp'=16,'dp'=8,'guide'=2] {'mp'}, dimensions={0} | all-to-all | bytes 786432 | tf_op jit(solution)/shard_map/all_to_all | solution.py:8
  154.9 0.7 reduce_sum.32
  (2 shorter events, 0.1 us)
Async XLA Ops:
  0.0 127.0 %copy-start = (bf16[896,512]{1,0:T(8,128)(2,1)S(1)}, bf16[896,512]{1,0:T(8,128)(2,1)}, u32[]{:S(2)}) copy-start(bf16[896,512]{1,0:T(8,128)(2,1)} %param.7) | copy-start | bytes 2752516
where the time goes:
time: 156 us
  blocking collectives  150 us (96%)
  matrix products  2.91 us (2%)
  other arithmetic  2.8 us (2%)
    all_gather x1, blocking collectives, per_device(): blocks = lax.all_gather(tokens, 'mp', axis=0, tiled=False)  70.5 us
    all_to_all x3, blocking collectives, summed_on_arrival(): lax.all_to_all(tiles, axis, split_axis=0, concat_axis=0, tiled=True)  62.6 us
    all_gather x1, blocking collectives, per_device(): hidden = lax.all_gather(hidden_share, ('dp', 'guide'), axis=0, tiled=True)  16.6 us

commit v1 on v0

--- a/solution.py
+++ b/solution.py
@@ -24,7 +24,8 @@
     chip_terms = summed_on_arrival(cut(partial_terms, guide), "guide").astype(jnp.bfloat16)
     summed = summed_on_arrival(cut(chip_terms, dp), "dp")
     hidden_share = (jax.nn.silu(summed[:, :columns]) * summed[:, columns:]).astype(jnp.bfloat16)
-    hidden = lax.all_gather(hidden_share, ("dp", "guide"), axis=0, tiled=True)
+    sent = jnp.stack([hidden_share] * lax.axis_size(("dp", "guide")))
+    hidden = jnp.concatenate(lax.all_to_all(sent, ("dp", "guide"), 0, 0), axis=0)
     output_terms = jnp.dot(hidden, w_down, preferred_element_type=jnp.float32).astype(jnp.bfloat16)
     return summed_on_arrival(cut(output_terms, mp), "mp").astype(jnp.bfloat16)
 

time: 156 us -> 164 us (1.051)
  blocking collectives: 150 us -> 158 us
    all_to_all x0 -> x1, blocking collectives: none -> 23.2 us  [per_device(): lax.all_to_all(sent, ('dp', 'guide'), 0, 0)]
    all_gather x1 -> x0, blocking collectives: 16.6 us -> none  [per_device(): hidden = lax.all_gather(hidden_share, ('dp', 'guide'), axis=0, tiled=True)]
    all_to_all x3, blocking collectives: 62.6 us -> 64.2 us  [summed_on_arrival(): lax.all_to_all(tiles, axis, split_axis=0, concat_axis=0, tiled=True)]
where the time goes in v1:
time: 164 us
  blocking collectives  158 us (96%)
  matrix products  2.91 us (2%)
  other arithmetic  2.8 us (2%)
    all_gather x1, blocking collectives, per_device(): blocks = lax.all_gather(tokens, 'mp', axis=0, tiled=False)  70.5 us
    all_to_all x3, blocking collectives, summed_on_arrival(): lax.all_to_all(tiles, axis, split_axis=0, concat_axis=0, tiled=True)  64.2 us
    all_to_all x1, blocking collectives, per_device(): lax.all_to_all(sent, ('dp', 'guide'), 0, 0)  23.2 us

profile of v1, /device:TPU:80, one launch (start us, length us, event | category | flops | bytes accessed | tf_op | source)
XLA Modules:
  0.0 163.8 jit_solution(2736902151666224511)
XLA Ops:
  0.0 0.0 copy-start
  0.0 70.5 %all-gather = bf16[384,512]{1,0:T(8,128)(2,1)S(1)} all-gather(bf16[24,512]{1,0:T(8,128)(2,1)} %param.4), channel_id=2, replica_groups=mesh['groups'=2,'mp'=16,'dp'=8,'guide'=2] {'mp'}, dimensions={0}, use_global_device_ids=true | all-gather | bytes 417792 | tf_op jit(solution)/shard_map/all_gather | solution.py:20
  70.6 2.3 %fusion = f32[1792,384]{0,1:T(8,128)S(1)} fusion(bf16[384,512]{1,0:T(8,128)(2,1)S(1)} %bitcast.15, bf16[512,896]{1,0:T(8,128)(2,1)} %param.6, bf16[512,896]{1,0:T(8,128)(2,1)} %param.5), kind=kOutput, calls=%fused_computation | convolution fusion | flops 708313088 | bytes 4980736 | tf_op jit(solution)/shard_map/dot_general | solution.py:23
  72.9 6.9 %all_to_all.20 = f32[2,192,1792]{2,1,0:T(8,128)} all-to-all(f32[2,192,1792]{2,1,0:T(8,128)S(1)} %bitcast.13), channel_id=1, replica_groups=mesh['groups'=2,'mp'=16,'dp'=8,'guide'=2] {'guide'}, dimensions={0} | all-to-all | bytes 5505024 | tf_op jit(solution)/shard_map/all_to_all | solution.py:8
  79.8 2.0 %reduce_sum.30 = bf16[192,1792]{1,0:T(8,128)(2,1)S(1)} reduce(f32[2,192,1792]{2,1,0:T(8,128)} %all_to_all.20, f32[]{:T(128)} %constant.4.clone.1), dimensions={0}, to_apply=%region_0.0 | reduce | flops 344064 | bytes 3440644 | tf_op jit(solution)/shard_map/reduce_sum | solution.py:9
  81.8 28.4 %all_to_all.21 = bf16[8,24,1792]{2,1,0:T(8,128)(2,1)S(1)} all-to-all(bf16[8,24,1792]{2,1,0:T(8,128)(2,1)S(1)} %bitcast.14), channel_id=1, replica_groups=mesh['groups'=2,'mp'=16,'dp'=8,'guide'=2] {'dp'}, dimensions={0} | all-to-all | bytes 1376256 | tf_op jit(solution)/shard_map/all_to_all | solution.py:8
  110.2 0.1 convert_reduce_fusion
  110.4 0.1 stack.2
  110.4 23.2 %all_to_all.22 = bf16[16,24,896]{2,1,0:T(8,128)(2,1)S(1)} all-to-all(bf16[16,24,896]{2,1,0:T(8,128)(2,1)S(1)} %stack.2), channel_id=1, replica_groups=mesh['groups'=2,'mp'=16,'dp'=8,'guide'=2] {'dp','guide'}, dimensions={0} | all-to-all | bytes 1376256 | tf_op jit(solution)/shard_map/all_to_all | solution.py:28
  133.6 0.0 copy-done
  133.6 0.6 convolution_convert_fusion
  134.2 28.9 %all_to_all.23 = bf16[16,24,512]{2,1,0:T(8,128)(2,1)S(1)} all-to-all(bf16[16,24,512]{2,1,0:T(8,128)(2,1)S(1)} %bitcast.18), channel_id=1, replica_groups=mesh['groups'=2,'mp'=16,'dp'=8,'guide'=2] {'mp'}, dimensions={0} | all-to-all | bytes 786432 | tf_op jit(solution)/shard_map/all_to_all | solution.py:8
  163.1 0.7 reduce_sum.32
  (2 shorter events, 0.1 us)
Async XLA Ops:
  0.0 133.6 %copy-start = (bf16[896,512]{1,0:T(8,128)(2,1)S(1)}, bf16[896,512]{1,0:T(8,128)(2,1)}, u32[]{:S(2)}) copy-start(bf16[896,512]{1,0:T(8,128)(2,1)} %param.7) | copy-start | bytes 2752516
